TPU v7x, 32 devices: a whole 2x2x4 slice. The times are simulated.
32 devices in a mesh: dp: 8 (over y, x, core), tensor: 4 (over z).
Axes of the slice: x: 2, y: 2, z: 4, core: 2. Of those that a mesh axis runs over, the one named last changes fastest.
Arguments:
- tokens: bfloat16 [8192, 2048], P('dp'), may hold values from -6 to 6
- attn_norm_gain: float32 [2048], replicated, may hold values from 0.5 to 1.5
- attn_norm_bias: float32 [2048], replicated, may hold values from -1.8 to 1.8
- mlp_norm_gain: float32 [2048], replicated, may hold values from 0.5 to 1.5
- mlp_norm_bias: float32 [2048], replicated, may hold values from -1.8 to 1.8
- w_qkv: bfloat16 [2048, 6144], P(None, 'tensor'), may hold values from -0.125 to 0.125
- qkv_bias: float32 [6144], P('tensor'), may hold values from -3 to 3
- w_out: bfloat16 [2048, 2048], P('tensor'), may hold values from -0.75 to 0.75
- w_up: bfloat16 [2048, 8192], P(None, 'tensor'), may hold values from -0.125 to 0.125
- up_bias: float32 [8192], P('tensor'), may hold values from -3 to 3
- w_down: bfloat16 [8192, 2048], P('tensor'), may hold values from -0.0625 to 0.0625
- out_bias: float32 [2048], replicated, may hold values from -3 to 3
- cotangent: bfloat16 [8192, 2048], P('dp'), may hold values from -6 to 6
Outputs:
- block_out: bfloat16 [8192, 2048], P('dp')
- input_grad: float32 [8192, 2048], P('dp')
- grad_w_qkv: float32 [2048, 6144], P('dp', 'tensor')
- grad_w_out: float32 [2048, 2048], P('tensor', 'dp')
- grad_w_up: float32 [2048, 8192], P('dp', 'tensor')
- grad_w_down: float32 [8192, 2048], P('tensor', 'dp')
- grad_norm_params: float32 [4, 2048], replicated
- grad_qkv_bias: float32 [6144], replicated
- grad_up_bias: float32 [8192], replicated
- grad_out_bias: float32 [2048], replicated
All inputs are finite; a program needn't handle non-finite values.
Results may differ from a plain program's by a relative error of at most 0.012.
Values may be sent and summed in bfloat16 or wider, within the bound.
A program may use at most 192 MiB of HBM per device.

v0:
```python
import jax
import jax.numpy as jnp
from jax import lax
from jax.sharding import PartitionSpec as P

H = 8
HD = 256
FF = 8192
ROT = 64
SEQ_LEN = 1024
EPSILON = 1e-05
ROPE_BASE = 10000.0
MASKED = -1e30


def layer_stats(tokens_f):
    row_mean = jnp.mean(tokens_f, axis=1, keepdims=True)
    centred = tokens_f - row_mean
    variance = jnp.mean(centred * centred, axis=1, keepdims=True)
    inv_std = lax.rsqrt(variance + EPSILON)
    return (centred * inv_std, inv_std)


def rotary_tables(length):
    half_rot = ROT // 2
    freqs = ROPE_BASE ** (-(2.0 * jnp.arange(half_rot, dtype=jnp.float32)) / ROT)
    angles = jnp.arange(length, dtype=jnp.float32)[:, None] * freqs[None, :]
    return (jnp.cos(angles), jnp.sin(angles))


def rotate(values, cosine_table, sine_table):
    half_rot = ROT // 2
    first_half = values[..., :half_rot]
    second_half = values[..., half_rot:ROT]
    cos_rows = cosine_table[:, None, :]
    sin_rows = sine_table[:, None, :]
    return jnp.concatenate(
        [
            first_half * cos_rows - second_half * sin_rows,
            second_half * cos_rows + first_half * sin_rows,
            values[..., ROT:],
        ],
        axis=-1,
    )


def unrotate(grads, cosine_table, sine_table):
    half_rot = ROT // 2
    first_half = grads[..., :half_rot]
    second_half = grads[..., half_rot:ROT]
    cos_rows = cosine_table[:, None, :]
    sin_rows = sine_table[:, None, :]
    return jnp.concatenate(
        [
            first_half * cos_rows + second_half * sin_rows,
            second_half * cos_rows - first_half * sin_rows,
            grads[..., ROT:],
        ],
        axis=-1,
    )


def masked_scores(query_block, keys_all, block_start):
    scaling = float(HD) ** (-0.5)
    scores = (
        jnp.einsum("sqhd,skhd->shqk", query_block, keys_all, preferred_element_type=jnp.float32)
        * scaling
    )
    query_pos = block_start + jnp.arange(query_block.shape[1])
    key_pos = jnp.arange(keys_all.shape[1])
    causal = key_pos[None, :] <= query_pos[:, None]
    return jnp.where(causal[None, None], scores, MASKED)


def attention_forward(queries, keys_all, values_all):
    length = queries.shape[1]
    block_rows = min(512, length)
    outputs = []
    log_parts = []
    for block_start in range(0, length, block_rows):
        query_block = queries[:, block_start : block_start + block_rows]
        scores = masked_scores(query_block, keys_all, block_start)
        row_top = jnp.max(scores, axis=-1, keepdims=True)
        log_total = row_top + jnp.log(jnp.sum(jnp.exp(scores - row_top), axis=-1, keepdims=True))
        soft_probs = jnp.exp(scores - log_total).astype(jnp.bfloat16)
        outputs.append(
            jnp.einsum(
                "shqk,skhd->sqhd", soft_probs, values_all, preferred_element_type=jnp.float32
            )
        )
        log_parts.append(log_total)
    return (jnp.concatenate(outputs, axis=1), jnp.concatenate(log_parts, axis=2))


def attention_backward(queries, keys_all, values_all, log_sums, grad_blocks):
    length = queries.shape[1]
    block_rows = min(512, length)
    scaling = float(HD) ** (-0.5)
    query_grads = []
    key_grad = jnp.zeros(keys_all.shape, jnp.float32)
    value_grad = jnp.zeros(values_all.shape, jnp.float32)
    for block_start in range(0, length, block_rows):
        query_block = queries[:, block_start : block_start + block_rows]
        grad_block = grad_blocks[:, block_start : block_start + block_rows]
        scores = masked_scores(query_block, keys_all, block_start)
        soft_probs = jnp.exp(scores - log_sums[:, :, block_start : block_start + block_rows])
        prob_grad = jnp.einsum(
            "sqhd,skhd->shqk", grad_block, values_all, preferred_element_type=jnp.float32
        )
        value_grad = value_grad + jnp.einsum(
            "shqk,sqhd->skhd",
            soft_probs.astype(jnp.bfloat16),
            grad_block,
            preferred_element_type=jnp.float32,
        )
        row_dot = jnp.sum(soft_probs * prob_grad, axis=-1, keepdims=True)
        score_grad = (soft_probs * (prob_grad - row_dot)).astype(jnp.bfloat16)
        query_grads.append(
            jnp.einsum("shqk,skhd->sqhd", score_grad, keys_all, preferred_element_type=jnp.float32)
            * scaling
        )
        key_grad = (
            key_grad
            + jnp.einsum(
                "shqk,sqhd->skhd", score_grad, query_block, preferred_element_type=jnp.float32
            )
            * scaling
        )
    return (jnp.concatenate(query_grads, axis=1), key_grad, value_grad)


def norm_back(seed_rows, scale_rows, normed_rows, grad_rows):
    grad_mean = jnp.mean(grad_rows, axis=1, keepdims=True)
    cross_mean = jnp.mean(grad_rows * normed_rows, axis=1, keepdims=True)
    return seed_rows.astype(jnp.float32) + scale_rows * (
        grad_rows - grad_mean - normed_rows * cross_mean
    )


def per_device(
    tokens,
    attn_norm_gain,
    attn_norm_bias,
    mlp_norm_gain,
    mlp_norm_bias,
    w_qkv,
    qkv_bias,
    w_out,
    w_up,
    up_bias,
    w_down,
    out_bias,
    cotangent,
):
    row_count = tokens.shape[0]
    seq_count = row_count // SEQ_LEN
    local_heads = w_qkv.shape[1] // (3 * HD)
    tokens_f = tokens.astype(jnp.float32)
    normed, inv_std = layer_stats(tokens_f)
    attn_in = (normed * attn_norm_gain + attn_norm_bias).astype(jnp.bfloat16)
    mlp_in = (normed * mlp_norm_gain + mlp_norm_bias).astype(jnp.bfloat16)
    projected = jnp.dot(attn_in, w_qkv, preferred_element_type=jnp.float32) + qkv_bias
    projected = projected.reshape(seq_count, SEQ_LEN, local_heads, 3, HD)
    cosine_table, sine_table = rotary_tables(SEQ_LEN)
    queries = rotate(projected[:, :, :, 0], cosine_table, sine_table).astype(jnp.bfloat16)
    keys_all = rotate(projected[:, :, :, 1], cosine_table, sine_table).astype(jnp.bfloat16)
    values_all = projected[:, :, :, 2].astype(jnp.bfloat16)
    attended, log_sums = attention_forward(queries, keys_all, values_all)
    attended = attended.astype(jnp.bfloat16).reshape(row_count, local_heads * HD)
    up_pre = jnp.dot(mlp_in, w_up, preferred_element_type=jnp.float32) + up_bias
    hidden = jax.nn.gelu(up_pre, approximate=False).astype(jnp.bfloat16)
    branch_terms = jnp.dot(attended, w_out, preferred_element_type=jnp.float32) + jnp.dot(
        hidden, w_down, preferred_element_type=jnp.float32
    )
    share_rows = row_count // lax.axis_size("tensor")
    row_start = lax.axis_index("tensor") * share_rows
    branch_total = lax.psum(branch_terms, "tensor")
    block_out = (tokens_f + branch_total + out_bias).astype(jnp.bfloat16)
    hidden_grad = jnp.einsum("td,fd->tf", cotangent, w_down, preferred_element_type=jnp.float32)
    gelu_pull = jax.vjp(lambda pre_act: jax.nn.gelu(pre_act, approximate=False), up_pre)[1]
    up_grad = gelu_pull(hidden_grad)[0].astype(jnp.bfloat16)
    grad_down_local = jnp.einsum("tf,td->fd", hidden, cotangent, preferred_element_type=jnp.float32)
    grad_up_local = jnp.einsum("tc,tf->cf", mlp_in, up_grad, preferred_element_type=jnp.float32)
    mlp_in_grad = jnp.einsum("tf,cf->tc", up_grad, w_up, preferred_element_type=jnp.float32)
    up_bias_grad = jnp.sum(up_grad, axis=0, dtype=jnp.float32)
    attended_grad = jnp.einsum("td,ed->te", cotangent, w_out, preferred_element_type=jnp.float32)
    attended_grad = attended_grad.astype(jnp.bfloat16)
    grad_out_local = jnp.einsum(
        "te,td->ed", attended, cotangent, preferred_element_type=jnp.float32
    )
    grad_blocks = attended_grad.reshape(seq_count, SEQ_LEN, local_heads, HD)
    query_grad, key_grad, value_grad = attention_backward(
        queries, keys_all, values_all, log_sums, grad_blocks
    )
    projected_grad = jnp.stack(
        [
            unrotate(query_grad, cosine_table, sine_table),
            unrotate(key_grad, cosine_table, sine_table),
            value_grad,
        ],
        axis=3,
    )
    projected_grad = projected_grad.reshape(row_count, local_heads * 3 * HD).astype(jnp.bfloat16)
    grad_qkv_local = jnp.einsum(
        "tc,te->ce", attn_in, projected_grad, preferred_element_type=jnp.float32
    )
    qkv_bias_grad = jnp.sum(projected_grad, axis=0, dtype=jnp.float32)
    attn_in_grad = jnp.einsum(
        "te,ce->tc", projected_grad, w_qkv, preferred_element_type=jnp.float32
    )
    grad_w_qkv, grad_w_out, grad_w_up, grad_w_down = (
        lax.psum_scatter(grad_qkv_local, "dp", scatter_dimension=0, tiled=True),
        lax.psum_scatter(grad_out_local, "dp", scatter_dimension=1, tiled=True),
        lax.psum_scatter(grad_up_local, "dp", scatter_dimension=0, tiled=True),
        lax.psum_scatter(grad_down_local, "dp", scatter_dimension=1, tiled=True),
    )
    norm_terms = jnp.stack(
        [
            jnp.sum(attn_in_grad * normed, axis=0),
            jnp.sum(attn_in_grad, axis=0),
            jnp.sum(mlp_in_grad * normed, axis=0),
            jnp.sum(mlp_in_grad, axis=0),
        ]
    )
    normed_part = attn_in_grad * attn_norm_gain + mlp_in_grad * mlp_norm_gain
    normed_grad = lax.psum(normed_part, "tensor")
    input_grad = norm_back(cotangent, inv_std, normed, normed_grad)
    tensor_index = lax.axis_index("tensor")
    qkv_full = lax.dynamic_update_slice(
        jnp.zeros((3 * H * HD,), jnp.float32),
        qkv_bias_grad,
        (tensor_index * qkv_bias_grad.shape[0],),
    )
    up_full = lax.dynamic_update_slice(
        jnp.zeros((FF,), jnp.float32), up_bias_grad, (tensor_index * up_bias_grad.shape[0],)
    )
    out_bias_part = jnp.sum(
        lax.dynamic_slice_in_dim(cotangent, row_start, share_rows, 0), axis=0, dtype=jnp.float32
    )
    grad_norm_params, grad_qkv_bias, grad_up_bias, grad_out_bias = lax.psum(
        (norm_terms, qkv_full, up_full, out_bias_part), ("dp", "tensor")
    )
    return (
        block_out,
        input_grad,
        grad_w_qkv,
        grad_w_out,
        grad_w_up,
        grad_w_down,
        grad_norm_params,
        grad_qkv_bias,
        grad_up_bias,
        grad_out_bias,
    )


def solution(mesh):
    placed = (
        P("dp", None),
        P(),
        P(),
        P(),
        P(),
        P(None, "tensor"),
        P("tensor"),
        P("tensor", None),
        P(None, "tensor"),
        P("tensor"),
        P("tensor", None),
        P(),
        P("dp", None),
    )
    return jax.shard_map(
        per_device,
        mesh=mesh,
        in_specs=placed,
        out_specs=(
            P("dp", None),
            P("dp", None),
            P("dp", "tensor"),
            P("tensor", "dp"),
            P("dp", "tensor"),
            P("tensor", "dp"),
            P(),
            P(),
            P(),
            P(),
        ),
        check_vma=False,
    )
```

profile of v0, /device:TPU:0, one launch (start us, length us, event | category | flops | bytes accessed | tf_op | source)
XLA Modules:
  0.0 1126.1 jit_solution(10098458001995248072)
XLA Ops:
  8.3 3.0 convert_reduce_fusion
  16.1 8.9 convolution_add_fusion
  25.1 6.6 copy.63
  31.6 4.8 fusion.66
  42.3 3.0 copy.100
  47.3 3.3 subtract_convert_fusion.1
  82.2 4.7 copy.83
  87.0 11.9 %fusion.72 = f32[1024,2048]{1,0:T(8,128)} fusion(bf16[1024,1536]{0,1:T(8,128)(2,1)} %bitcast.118, bf16[2048,1536]{1,0:T(8,128)(2,1)} %param.18), kind=kOutput, calls=%fused_computation.135 | convolution fusion | flops 6442450944 | bytes 17825792 | tf_op jit(solution)/shard_map/te,ce->tc/dot_general | solution.py:208
  99.0 11.8 %fusion.59 = f32[1024,2048]{1,0:T(8,128)S(1)} fusion(bf16[2048,2048]{1,0:T(8,128)(2,1)} %param.21, bf16[1024,2048]{1,0:T(8,128)(2,1)S(1)} %copy-done.2, f32[2048]{0:T(1024)S(1)} %copy-done.27, f32[2048]{0:T(1024)S(1)} %copy-done.29, f32[1024]{0:T(1024)S(1)} %add_rsqrt_fusion, f32[1024]{0:T(1024)S(1)} %broadcast_multiply_fusion.2), kind=kOutput, calls=%fused_computation.130 | convolution fusion | flops 8602517504 | bytes 20996096 | tf_op jit(solution)/shard_map/dot_general | solution.py:170
  110.8 29.3 %convert_reduce_fusion.1 = (f32[2048]{0:T(1024)S(1)}, bf16[1024,2048]{1,0:T(8,128)(2,1)}, f32[1024,2048]{1,0:T(8,128)}) fusion(f32[1024,2048]{1,0:T(8,128)S(1)} %fusion.59, f32[2048]{0:T(1024)S(1)} %copy-done.19, bf16[1024,2048]{1,0:T(8,128)(2,1)S(1)} %copy-done.5, bf16[2048,2048]{1,0:T(8,128)(2,1)S(1)} %bitcast.133), kind=kOutput, calls=%fused_computation.26 | convolution fusion | flops 8747218944 | bytes 33570816 | tf_op jit(solution)/shard_map/td,fd->tf/dot_general | solution.py:179
  140.1 8.0 multiply_convert_fusion
  148.1 14.7 %fusion.71 = f32[1024,2048]{1,0:T(8,128)} fusion(bf16[1024,2048]{1,0:T(8,128)(2,1)S(1)} %multiply_convert_fusion, bf16[2048,2048]{1,0:T(8,128)(2,1)} %param.23), kind=kOutput, calls=%fused_computation.134 | convolution fusion | flops 8589934592 | bytes 20971520 | tf_op jit(solution)/shard_map/dot_general | solution.py:172
  162.9 17.1 %multiply_add_fusion = (f32[1024,2048]{1,0:T(8,128)}, f32[1024,2048]{1,0:T(8,128)}) fusion(f32[1024,2048]{1,0:T(8,128)} %fusion.72, f32[2048]{0:T(1024)S(1)} %copy-done.29, f32[2048]{0:T(1024)S(1)} %copy-done.26, bf16[1024,2048]{1,0:T(8,128)(2,1)} %get-tuple-element.27, bf16[2048,2048]{1,0:T(8,128)(2,1)} %param.21), kind=kOutput, calls=%fused_computation.27 | convolution fusion | flops 8596226048 | bytes 37765120 | tf_op jit(solution)/shard_map/tf,cf->tc/dot_general | solution.py:184
  180.0 9.2 convolution_add_fusion.1
  189.3 6.5 fusion.40
  199.8 554.5 %all-reduce.7.cloned.1.call-done = (f32[1024,2048]{1,0:T(8,128)}, f32[1024,2048]{1,0:T(8,128)}) async-done(((f32[1024,2048]{1,0:T(8,128)}, f32[1024,2048]{1,0:T(8,128)}), (f32[1024,2048]{1,0:T(8,128)}, f32[1024,2048]{1,0:T(8,128)})) %all-reduce.7.cloned.1.call-update) | async-done | bytes 16777232 | tf_op jit(solution)/shard_map/psum | solution.py:177
  754.3 11.8 %fusion.64 = (f32[1024]{0:T(1024)S(1)}, f32[1024]{0:T(1024)S(1)}, f32[2048]{0:T(1024)S(1)}, f32[2048]{0:T(1024)S(1)}, f32[2048]{0:T(1024)S(1)}, /*index=5*/f32[2048]{0:T(1024)S(1)}) fusion(f32[1024,2048]{1,0:T(8,128)} %get-tuple-element.25, f32[1024]{0:T(1024)S(1)} %copy-done.17, f32[1024]{0:T(1024)S(1)} %copy-done.15, bf16[1024,2048]{1,0:T(8,128)(2,1)} %param.13, ...), kind=kLoop, calls=%fused_computation.132 | loop fusion | flops 25155584 | bytes 29409280 | tf_op jit(solution)/shard_map/reduce_sum | solution.py:133
  766.9 14.5 %fusion.61 = f32[2048,1536]{1,0:T(8,128)} fusion(bf16[1024,1536]{0,1:T(8,128)(2,1)} %bitcast.119, bf16[1024,2048]{1,0:T(8,128)(2,1)} %param.13, f32[2048]{0:T(1024)S(1)} %copy-done.24, f32[2048]{0:T(1024)S(1)} %copy-done.26, f32[1024]{0:T(1024)S(1)} %copy-done.17, f32[1024]{0:T(1024)S(1)} %copy-done.15), kind=kOutput, calls=%fused_computation.131 | convolution fusion | flops 6455033856 | bytes 19947520 | tf_op jit(solution)/shard_map/tc,te->ce/dot_general | solution.py:204
  781.5 17.7 %fusion.73 = f32[2048,2048]{1,0:T(8,128)} fusion(bf16[1024,2048]{1,0:T(8,128)(2,1)} %copy-done.8, bf16[1024,2048]{1,0:T(8,128)(2,1)} %param.25), kind=kOutput, calls=%fused_computation.136 | convolution fusion | flops 8589934592 | bytes 25165824 | tf_op jit(solution)/shard_map/tf,td->fd/dot_general | solution.py:182
  799.9 15.9 %fusion.57 = f32[2048,2048]{1,0:T(8,128)} fusion(bf16[1024,2048]{1,0:T(8,128)(2,1)} %get-tuple-element.27, bf16[1024,2048]{1,0:T(8,128)(2,1)} %param.13, f32[2048]{0:T(1024)S(1)} %copy-done.28, f32[2048]{0:T(1024)S(1)} %copy-done.29, f32[1024]{0:T(1024)S(1)} %copy-done.17, f32[1024]{0:T(1024)S(1)} %copy-done.15), kind=kOutput, calls=%fused_computation.129 | convolution fusion | flops 8602517504 | bytes 25190400 | tf_op jit(solution)/shard_map/tc,tf->cf/dot_general | solution.py:183
  816.5 16.0 %fusion.15 = (f32[1024,2048]{1,0:T(8,128)}, bf16[1024,2048]{1,0:T(8,128)(2,1)}) fusion(bf16[1024,2048]{1,0:T(8,128)(2,1)} %param.13, f32[1024,2048]{1,0:T(8,128)} %get-tuple-element.25, bf16[1024,2048]{1,0:T(8,128)(2,1)} %param.25, f32[1024]{0:T(1024)S(1)} %broadcast_multiply_fusion, f32[1024]{0:T(1024)S(1)} %broadcast_multiply_fusion.1, ...), kind=kLoop, calls=%fused_computation.19 | loop fusion | flops 25165824 | bytes 37773312 | tf_op jit(solution)/shard_map/add | solution.py:135
  832.5 73.3 %all-reduce.5.cloned.1.call-done = (f32[4,2048]{1,0:T(4,128)}, f32[6144]{0:T(1024)}, f32[8192]{0:T(1024)}, f32[2048]{0:T(1024)}) async-done(((f32[4,2048]{1,0:T(4,128)}, f32[6144]{0:T(1024)}, f32[8192]{0:T(1024)}, f32[2048]{0:T(1024)}), (f32[4,2048]{1,0:T(4,128)}, f32[6144]{0:T(1024)}, f32[8192]{0:T(1024)}, f32[2048]{0:T(1024)})) %all-reduce.5.cloned.1.call-update) | async-done | bytes 98320 | tf_op jit(solution)/shard_map/psum | solution.py:240
  905.8 86.9 %reduce-scatter.11.cloned.1.call-done = f32[2048,256]{1,0:T(8,128)} async-done(((f32[2048,2048]{1,0:T(8,128)}), f32[2048,256]{1,0:T(8,128)}) %reduce-scatter.11.cloned.1.call-update) | async-done | bytes 2097168 | tf_op jit(solution)/shard_map/reduce_scatter | solution.py:215
  992.7 120.2 %reduce-scatter.9.cloned.1.call-done = f32[256,2048]{1,0:T(8,128)} async-done(((f32[2048,2048]{1,0:T(8,128)}), f32[256,2048]{1,0:T(8,128)}) %reduce-scatter.9.cloned.1.call-update) | async-done | bytes 2097168 | tf_op jit(solution)/shard_map/reduce_scatter | solution.py:214
  (134 shorter events, 56.0 us)
Async XLA Ops:
  8.0 49.0 %copy-start = (bf16[512,2048]{1,0:T(8,128)(2,1)S(1)}, bf16[512,2048]{1,0:T(8,128)(2,1)}, u32[]{:S(2)}) copy-start(bf16[512,2048]{1,0:T(8,128)(2,1)} %param.20) | copy-start | bytes 6291460
  8.0 746.3 %all-reduce.7.cloned.1.call-start = ((), (), s32[]{:S(2)}) async-start(), calls=%async_computation.9 | async-start | bytes 33554432 | tf_op jit(solution)/shard_map/psum | solution.py:177
  11.7 87.2 %copy-start.14 = (f32[1024]{0:T(1024)}, f32[1024]{0:T(1024)S(1)}, u32[]{:S(2)}) copy-start(f32[1024]{0:T(1024)S(1)} %broadcast_multiply_fusion.2) | copy-start | bytes 12292
  12.9 86.0 %copy-start.16 = (f32[1024]{0:T(1024)}, f32[1024]{0:T(1024)S(1)}, u32[]{:S(2)}) copy-start(f32[1024]{0:T(1024)S(1)} %add_rsqrt_fusion) | copy-start | bytes 12292
  86.9 11.9 %copy-start.2 = (bf16[1024,2048]{1,0:T(8,128)(2,1)S(1)}, bf16[1024,2048]{1,0:T(8,128)(2,1)}, u32[]{:S(2)}) copy-start(bf16[1024,2048]{1,0:T(8,128)(2,1)} %param.13) | copy-start | bytes 12582916
  86.9 12.0 %copy-start.27 = (f32[2048]{0:T(1024)S(1)}, f32[2048]{0:T(1024)}, u32[]{:S(2)}) copy-start(f32[2048]{0:T(1024)} %param.17) | copy-start | bytes 24580
  86.9 12.0 %copy-start.29 = (f32[2048]{0:T(1024)S(1)}, f32[2048]{0:T(1024)}, u32[]{:S(2)}) copy-start(f32[2048]{0:T(1024)} %param.16) | copy-start | bytes 24580
  87.0 23.8 %slice-start.2 = ((s8[8388608]{0:T(1024)(128)(4,1)}), s8[4194304]{0:T(1024)(128)(4,1)S(1)}, s32[]{:S(2)}) async-start(s8[8388608]{0:T(1024)(128)(4,1)} %bitcast.132), calls=%async_computation.12 | async-start | bytes 8388608
  98.9 11.9 %copy-start.5 = (bf16[1024,2048]{1,0:T(8,128)(2,1)S(1)}, bf16[1024,2048]{1,0:T(8,128)(2,1)}, u32[]{:S(2)}) copy-start(bf16[1024,2048]{1,0:T(8,128)(2,1)} %param.25) | copy-start | bytes 12582916
  110.8 29.3 %copy-start.3 = (f32[1024,2048]{1,0:T(8,128)}, f32[1024,2048]{1,0:T(8,128)S(1)}, u32[]{:S(2)}) copy-start(f32[1024,2048]{1,0:T(8,128)S(1)} %fusion.59) | copy-start | bytes 25165828
  148.1 14.8 %copy-start.8 = (bf16[1024,2048]{1,0:T(8,128)(2,1)}, bf16[1024,2048]{1,0:T(8,128)(2,1)S(1)}, u32[]{:S(2)}) copy-start(bf16[1024,2048]{1,0:T(8,128)(2,1)S(1)} %multiply_convert_fusion) | copy-start | bytes 12582916
  148.1 14.7 %copy-start.26 = (f32[2048]{0:T(1024)S(1)}, f32[2048]{0:T(1024)}, u32[]{:S(2)}) copy-start(f32[2048]{0:T(1024)} %param.14) | copy-start | bytes 24580
  162.9 17.1 %copy-start.10 = (bf16[2,256,512]{2,1,0:T(8,128)(2,1)S(1)}, bf16[2,256,512]{2,1,0:T(8,128)(2,1)}, u32[]{:S(2)}) copy-start(bf16[2,256,512]{2,1,0:T(8,128)(2,1)} %convolution_convert_fusion.1) | copy-start | bytes 1572868
  162.9 17.1 %copy-start.11 = (bf16[2,256,512]{2,1,0:T(8,128)(2,1)S(1)}, bf16[2,256,512]{2,1,0:T(8,128)(2,1)}, u32[]{:S(2)}) copy-start(bf16[2,256,512]{2,1,0:T(8,128)(2,1)} %convolution_convert_fusion.2) | copy-start | bytes 1572868
  189.2 643.2 %reduce-scatter.7.cloned.1.call-start = ((), (), s32[]{:S(2)}) async-start(), calls=%async_computation.5 | async-start | bytes 4718592 | tf_op jit(solution)/shard_map/reduce_scatter | solution.py:213
  195.7 558.6 %copy-start.15 = (f32[1024]{0:T(1024)S(1)}, f32[1024]{0:T(1024)}, u32[]{:S(2)}) copy-start(f32[1024]{0:T(1024)} %copy-done.14) | copy-start | bytes 12292
  195.7 558.6 %copy-start.17 = (f32[1024]{0:T(1024)S(1)}, f32[1024]{0:T(1024)}, u32[]{:S(2)}) copy-start(f32[1024]{0:T(1024)} %copy-done.16) | copy-start | bytes 12292
  195.8 710.0 %all-reduce.5.cloned.1.call-start = ((), (), s32[]{:S(2)}) async-start(), calls=%async_computation.8 | async-start | bytes 196608 | tf_op jit(solution)/shard_map/psum | solution.py:240
  197.2 569.0 %copy-start.13 = (f32[6144]{0:T(1024)}, f32[6144]{0:T(1024)S(1)}, u32[]{:S(2)}) copy-start(f32[6144]{0:T(1024)S(1)} %dynamic_update_slice.6) | copy-start | bytes 73732
  197.5 568.6 %copy-start.12 = (f32[8192]{0:T(1024)}, f32[8192]{0:T(1024)S(1)}, u32[]{:S(2)}) copy-start(f32[8192]{0:T(1024)S(1)} %dynamic_update_slice.7) | copy-start | bytes 98308
  754.3 12.5 %copy-start.24 = (f32[2048]{0:T(1024)S(1)}, f32[2048]{0:T(1024)}, u32[]{:S(2)}) copy-start(f32[2048]{0:T(1024)} %param.15) | copy-start | bytes 24580
  766.8 138.9 %reduce-scatter.5.cloned.1.call-start = ((), (), s32[]{:S(2)}) async-start(), calls=%async_computation.4 | async-start | bytes 14155776 | tf_op jit(solution)/shard_map/reduce_scatter | solution.py:212
  781.4 211.3 %reduce-scatter.11.cloned.1.call-start = ((), (), s32[]{:S(2)}) async-start(), calls=%async_computation.7 | async-start | bytes 18874368 | tf_op jit(solution)/shard_map/reduce_scatter | solution.py:215
  799.2 313.7 %reduce-scatter.9.cloned.1.call-start = ((), (), s32[]{:S(2)}) async-start(), calls=%async_computation.6 | async-start | bytes 18874368 | tf_op jit(solution)/shard_map/reduce_scatter | solution.py:214
  (16 other events, 75.4 us)
Sparse Core Ops, SparseCore 0:
  189.3 564.9 all-reduce.6
  766.9 138.7 all-reduce.4
Sparse Core Ops, SparseCore 1:
  195.8 53.6 reduce-scatter.6
  781.5 91.2 reduce-scatter.4
  876.8 115.9 reduce-scatter.10
  996.9 116.0 reduce-scatter.8
where the time goes:
time: 1130 us
  waiting for transfers between devices  835 us (74%)
  matrix products  176 us (16%)
  other arithmetic  62 us (5%)
  local copies, waits for them, and re-layouts  36.2 us (3%)
  between operations  16.4 us (1%)
    psum x1, waiting for transfers between devices, per_device(): branch_total = lax.psum(branch_terms, 'tensor')  555 us
    reduce_scatter x1, waiting for transfers between devices, per_device(): lax.psum_scatter(grad_up_local, 'dp', scatter_dimension=0, tiled=True)  120 us
    reduce_scatter x1, waiting for transfers between devices, per_device(): lax.psum_scatter(grad_down_local, 'dp', scatter_dimension=1, tiled=True)  86.9 us
    psum x1, waiting for transfers between devices, per_device(): lax.psum((norm_terms, qkv_full, up_full, out_bias_part), ('dp', 'tensor'))  73.3 us
    dot_general x1, matrix products, per_device(): jnp.einsum('td,fd->tf', cotangent, w_down, preferred_element_type=jnp.flo...  29.3 us
  transfers between devices with their start and end apart: 6, of which 4 were waited for; matrix products, arithmetic and copies ran while one was open for 8% of the time, Pallas kernels for 0%

commit v1 on v0

--- a/solution.py
+++ b/solution.py
@@ -174,7 +174,7 @@
     )
     share_rows = row_count // lax.axis_size("tensor")
     row_start = lax.axis_index("tensor") * share_rows
-    branch_total = lax.psum(branch_terms, "tensor")
+    branch_total = jnp.sum(lax.all_gather(branch_terms, "tensor"), axis=0)
     block_out = (tokens_f + branch_total + out_bias).astype(jnp.bfloat16)
     hidden_grad = jnp.einsum("td,fd->tf", cotangent, w_down, preferred_element_type=jnp.float32)
     gelu_pull = jax.vjp(lambda pre_act: jax.nn.gelu(pre_act, approximate=False), up_pre)[1]

time: 1130 us -> 1160 us (1.027)
  other arithmetic: 62 us -> 78.9 us
    all_gather x0 -> x1, waiting for transfers between devices: none -> 498 us  [per_device(): branch_total = jnp.sum(lax.all_gather(branch_terms, 'tensor'), axis=0)]
    psum x1, waiting for transfers between devices: 555 us -> 246 us  [per_device(): normed_grad = lax.psum(normed_part, 'tensor')]
    reduce_scatter x1, waiting for transfers between devices: 120 us -> 0.01 us  [per_device(): lax.psum_scatter(grad_up_local, 'dp', scatter_dimension=0, tiled=True)]
    reduce_scatter x1, waiting for transfers between devices: 86.9 us -> 0.01 us  [per_device(): lax.psum_scatter(grad_down_local, 'dp', scatter_dimension=1, tiled=True)]
    psum x1, waiting for transfers between devices: 73.3 us -> 98.3 us  [per_device(): lax.psum((norm_terms, qkv_full, up_full, out_bias_part), ('dp', 'tensor'))]
    reduce_sum x0 -> x1, other arithmetic: none -> 16.1 us  [per_device(): branch_total = jnp.sum(lax.all_gather(branch_terms, 'tensor'), axis=0)]
  transfers between devices with their start and end apart: 6 -> 7, of which waited for: 4 -> 3; matrix products, arithmetic and copies ran while one was open for 8% -> 12% of each run, Pallas kernels for 0% -> 0%
where the time goes in v1:
time: 1160 us; the launch traced here: 1150 us
  waiting for transfers between devices  842 us (73%)
  matrix products  179 us (15%)
  other arithmetic  78.9 us (7%)
  local copies, waits for them, and re-layouts  37.5 us (3%)
  between operations  16.3 us (1%)
    all_gather x1, waiting for transfers between devices, per_device(): branch_total = jnp.sum(lax.all_gather(branch_terms, 'tensor'), axis=0)  498 us
    psum x1, waiting for transfers between devices, per_device(): normed_grad = lax.psum(normed_part, 'tensor')  246 us
    psum x1, waiting for transfers between devices, per_device(): lax.psum((norm_terms, qkv_full, up_full, out_bias_part), ('dp', 'tensor'))  98.3 us
    dot_general x1, matrix products, per_device(): jnp.einsum('td,fd->tf', cotangent, w_down, preferred_element_type=jnp.flo...  29.3 us
  transfers between devices with their start and end apart: 7, of which 3 were waited for; matrix products, arithmetic and copies ran while one was open for 12% of the time, Pallas kernels for 0%

profile of v1, /device:TPU:0, one launch (start us, length us, event | category | flops | bytes accessed | tf_op | source)
XLA Modules:
  0.0 1154.4 jit_solution(6274559366605380828)
XLA Ops:
  15.8 11.5 %convolution_add_fusion = f32[1024,1536]{1,0:T(8,128)} fusion(bf16[2048,1536]{1,0:T(8,128)(2,1)} %param.18, f32[1536]{0:T(1024)S(1)} %copy-done.33, bf16[1024,2048]{1,0:T(8,128)(2,1)S(1)} %copy-done.1, f32[2048]{0:T(1024)S(1)} %copy-done.34, f32[2048]{0:T(1024)S(1)} %copy-done.36, f32[1024]{0:T(1024)S(1)} %add_rsqrt_fusion, ...), kind=kOutput, calls=%fused_computation.45 | convolution fusion | flops 6456606720 | bytes 16807936 | tf_op jit(solution)/shard_map/dot_general | solution.py:162
  27.4 6.6 copy.63
  34.0 4.8 fusion.66
  49.7 3.2 subtract_convert_fusion.1
  81.4 4.7 copy.83
  86.1 12.0 %fusion.72 = f32[1024,2048]{1,0:T(8,128)} fusion(bf16[1024,1536]{0,1:T(8,128)(2,1)} %bitcast.120, bf16[2048,1536]{1,0:T(8,128)(2,1)} %param.18), kind=kOutput, calls=%fused_computation.135 | convolution fusion | flops 6442450944 | bytes 17825792 | tf_op jit(solution)/shard_map/te,ce->tc/dot_general | solution.py:208
  98.1 11.8 %fusion.59 = f32[1024,2048]{1,0:T(8,128)S(1)} fusion(bf16[2048,2048]{1,0:T(8,128)(2,1)} %param.21, bf16[1024,2048]{1,0:T(8,128)(2,1)S(1)} %copy-done.2, f32[2048]{0:T(1024)S(1)} %copy-done.39, f32[2048]{0:T(1024)S(1)} %copy-done.38, f32[1024]{0:T(1024)S(1)} %add_rsqrt_fusion, f32[1024]{0:T(1024)S(1)} %broadcast_multiply_fusion.2), kind=kOutput, calls=%fused_computation.130 | convolution fusion | flops 8602517504 | bytes 20996096 | tf_op jit(solution)/shard_map/dot_general | solution.py:170
  110.0 29.3 %convert_reduce_fusion.1 = (f32[2048]{0:T(1024)S(1)}, bf16[1024,2048]{1,0:T(8,128)(2,1)}, f32[1024,2048]{1,0:T(8,128)}) fusion(f32[1024,2048]{1,0:T(8,128)S(1)} %fusion.59, f32[2048]{0:T(1024)S(1)} %copy-done.31, bf16[1024,2048]{1,0:T(8,128)(2,1)S(1)} %copy-done.12, bf16[2048,2048]{1,0:T(8,128)(2,1)S(1)} %bitcast.135), kind=kOutput, calls=%fused_computation.26 | convolution fusion | flops 8747218944 | bytes 33570816 | tf_op jit(solution)/shard_map/td,fd->tf/dot_general | solution.py:179
  139.4 17.2 %multiply_add_fusion = (f32[1024,2048]{1,0:T(8,128)}, f32[1024,2048]{1,0:T(8,128)}) fusion(f32[1024,2048]{1,0:T(8,128)} %fusion.72, f32[2048]{0:T(1024)S(1)} %copy-done.38, f32[2048]{0:T(1024)S(1)} %copy-done.37, bf16[1024,2048]{1,0:T(8,128)(2,1)} %get-tuple-element.25, bf16[2048,2048]{1,0:T(8,128)(2,1)} %param.21), kind=kOutput, calls=%fused_computation.27 | convolution fusion | flops 8596226048 | bytes 37765120 | tf_op jit(solution)/shard_map/tf,cf->tc/dot_general | solution.py:184
  157.6 5.1 convolution_convert_fusion.1
  162.7 3.8 convolution_convert_fusion.2
  166.5 8.0 multiply_convert_fusion
  174.5 12.8 %fusion.71 = f32[1024,2048]{1,0:T(8,128)S(1)} fusion(bf16[1024,2048]{1,0:T(8,128)(2,1)S(1)} %multiply_convert_fusion, bf16[2048,2048]{1,0:T(8,128)(2,1)} %param.23), kind=kOutput, calls=%fused_computation.134 | convolution fusion | flops 8589934592 | bytes 20971520 | tf_op jit(solution)/shard_map/dot_general | solution.py:172
  187.3 5.9 convolution_add_fusion.1
  194.4 6.5 fusion.40
  204.3 246.0 %all-reduce.4.cloned.1.call-done = f32[1024,2048]{1,0:T(8,128)} async-done(((f32[1024,2048]{1,0:T(8,128)}), f32[1024,2048]{1,0:T(8,128)}) %all-reduce.4.cloned.1.call-update) | async-done | bytes 8388624 | tf_op jit(solution)/shard_map/psum | solution.py:226
  450.3 14.1 %fusion.64 = (f32[1024]{0:T(1024)S(1)}, f32[1024]{0:T(1024)S(1)}, f32[2048]{0:T(1024)S(1)}, f32[2048]{0:T(1024)S(1)}, f32[2048]{0:T(1024)S(1)}, /*index=5*/f32[2048]{0:T(1024)S(1)}) fusion(f32[1024,2048]{1,0:T(8,128)} %all-reduce.4.cloned.1.call-done, f32[1024]{0:T(1024)S(1)} %copy-done.29, f32[1024]{0:T(1024)S(1)} %copy-done.23, ...), kind=kLoop, calls=%fused_computation.132 | loop fusion | flops 25155584 | bytes 29409280 | tf_op jit(solution)/shard_map/reduce_sum | solution.py:133
  465.1 15.3 %fusion.61 = f32[2048,1536]{1,0:T(8,128)} fusion(bf16[1024,1536]{0,1:T(8,128)(2,1)} %bitcast.121, bf16[1024,2048]{1,0:T(8,128)(2,1)} %param.13, f32[2048]{0:T(1024)S(1)} %copy-done.35, f32[2048]{0:T(1024)S(1)} %copy-done.37, f32[1024]{0:T(1024)S(1)} %copy-done.29, f32[1024]{0:T(1024)S(1)} %copy-done.23), kind=kOutput, calls=%fused_computation.131 | convolution fusion | flops 6455033856 | bytes 19947520 | tf_op jit(solution)/shard_map/tc,te->ce/dot_general | solution.py:204
  480.5 17.4 %fusion.73 = f32[2048,2048]{1,0:T(8,128)} fusion(bf16[1024,2048]{1,0:T(8,128)(2,1)} %copy-done.14, bf16[1024,2048]{1,0:T(8,128)(2,1)} %param.25), kind=kOutput, calls=%fused_computation.136 | convolution fusion | flops 8589934592 | bytes 25165824 | tf_op jit(solution)/shard_map/tf,td->fd/dot_general | solution.py:182
  498.6 15.9 %fusion.57 = f32[2048,2048]{1,0:T(8,128)} fusion(bf16[1024,2048]{1,0:T(8,128)(2,1)} %get-tuple-element.25, bf16[1024,2048]{1,0:T(8,128)(2,1)} %param.13, f32[2048]{0:T(1024)S(1)} %copy-done.40, f32[2048]{0:T(1024)S(1)} %copy-done.38, f32[1024]{0:T(1024)S(1)} %copy-done.29, f32[1024]{0:T(1024)S(1)} %copy-done.23), kind=kOutput, calls=%fused_computation.129 | convolution fusion | flops 8602517504 | bytes 25190400 | tf_op jit(solution)/shard_map/tc,tf->cf/dot_general | solution.py:183
  514.5 497.7 %all-gather.3.cloned.1.call-done = f32[4096,2048]{1,0:T(8,128)} async-done(((f32[1024,2048]{1,0:T(8,128)}), f32[4096,2048]{1,0:T(8,128)}) %all-gather.3.cloned.1.call-update) | async-done | bytes 33554448 | tf_op jit(solution)/shard_map/all_gather | solution.py:177
  1012.2 16.1 %reduce_sum.150 = f32[1024,2048]{1,0:T(8,128)} reduce(f32[4,1024,2048]{2,1,0:T(8,128)} %bitcast.115, f32[]{:T(128)} %constant.47.clone.1), dimensions={0}, to_apply=%region_6.7 | reduce | flops 6291456 | bytes 41943044 | tf_op jit(solution)/shard_map/reduce_sum | solution.py:177
  1028.4 14.8 %fusion.15 = (f32[1024,2048]{1,0:T(8,128)}, bf16[1024,2048]{1,0:T(8,128)(2,1)}) fusion(bf16[1024,2048]{1,0:T(8,128)(2,1)} %param.13, f32[1024,2048]{1,0:T(8,128)} %all-reduce.4.cloned.1.call-done, bf16[1024,2048]{1,0:T(8,128)(2,1)} %param.25, f32[1024]{0:T(1024)S(1)} %broadcast_multiply_fusion, f32[1024]{0:T(1024)S(1)} %broadcast_multiply_fusion.1, ...), kind=kLoop, calls=%fused_computation.19 | loop fusion | flops 25165824 | bytes 37773312 | tf_op jit(solution)/shard_map/add | solution.py:135
  1043.2 98.3 %all-reduce.6.cloned.1.call-done = (f32[4,2048]{1,0:T(4,128)}, f32[6144]{0:T(1024)}, f32[8192]{0:T(1024)}, f32[2048]{0:T(1024)}) async-done(((f32[4,2048]{1,0:T(4,128)}, f32[6144]{0:T(1024)}, f32[8192]{0:T(1024)}, f32[2048]{0:T(1024)}), (f32[4,2048]{1,0:T(4,128)}, f32[6144]{0:T(1024)}, f32[8192]{0:T(1024)}, f32[2048]{0:T(1024)})) %all-reduce.6.cloned.1.call-update) | async-done | bytes 98320 | tf_op jit(solution)/shard_map/psum | solution.py:240
  (160 shorter events, 59.5 us)
Async XLA Ops:
  8.0 49.1 %copy-start = (bf16[512,2048]{1,0:T(8,128)(2,1)S(1)}, bf16[512,2048]{1,0:T(8,128)(2,1)}, u32[]{:S(2)}) copy-start(bf16[512,2048]{1,0:T(8,128)(2,1)} %param.20) | copy-start | bytes 6291460
  8.0 442.3 %all-reduce.4.cloned.1.call-start = ((), (), s32[]{:S(2)}) async-start(), calls=%async_computation.4 | async-start | bytes 16777216 | tf_op jit(solution)/shard_map/psum | solution.py:226
  8.3 55.3 %copy-start.7 = (pred[512,1024]{1,0:T(8,128)(4,1)}, pred[512,1024]{1,0:T(8,128)(4,1)S(1)}, u32[]{:S(2)}) copy-start(pred[512,1024]{1,0:T(8,128)(4,1)S(1)} %iota_compare_fusion.2) | copy-start | bytes 1572868
  11.9 86.2 %copy-start.22 = (f32[1024]{0:T(1024)}, f32[1024]{0:T(1024)S(1)}, u32[]{:S(2)}) copy-start(f32[1024]{0:T(1024)S(1)} %broadcast_multiply_fusion.2) | copy-start | bytes 12292
  13.1 85.0 %copy-start.28 = (f32[1024]{0:T(1024)}, f32[1024]{0:T(1024)S(1)}, u32[]{:S(2)}) copy-start(f32[1024]{0:T(1024)S(1)} %add_rsqrt_fusion) | copy-start | bytes 12292
  86.1 12.0 %copy-start.39 = (f32[2048]{0:T(1024)S(1)}, f32[2048]{0:T(1024)}, u32[]{:S(2)}) copy-start(f32[2048]{0:T(1024)} %param.17) | copy-start | bytes 24580
  86.1 23.9 %slice-start.2 = ((s8[8388608]{0:T(1024)(128)(4,1)}), s8[4194304]{0:T(1024)(128)(4,1)S(1)}, s32[]{:S(2)}) async-start(s8[8388608]{0:T(1024)(128)(4,1)} %bitcast.134), calls=%async_computation.13 | async-start | bytes 8388608
  110.0 29.3 %copy-start.6 = (f32[1024,2048]{1,0:T(8,128)}, f32[1024,2048]{1,0:T(8,128)S(1)}, u32[]{:S(2)}) copy-start(f32[1024,2048]{1,0:T(8,128)S(1)} %fusion.59) | copy-start | bytes 25165828
  110.0 29.3 %copy-start.37 = (f32[2048]{0:T(1024)S(1)}, f32[2048]{0:T(1024)}, u32[]{:S(2)}) copy-start(f32[2048]{0:T(1024)} %param.14) | copy-start | bytes 24580
  156.6 855.7 %all-gather.3.cloned.1.call-start = ((), (), s32[]{:S(2)}) async-start(), calls=%async_computation.9 | async-start | bytes 41943040 | tf_op jit(solution)/shard_map/all_gather | solution.py:177
  174.5 12.8 %copy-start.14 = (bf16[1024,2048]{1,0:T(8,128)(2,1)}, bf16[1024,2048]{1,0:T(8,128)(2,1)S(1)}, u32[]{:S(2)}) copy-start(bf16[1024,2048]{1,0:T(8,128)(2,1)S(1)} %multiply_convert_fusion) | copy-start | bytes 12582916
  174.5 12.8 %copy-start.16 = (bf16[2,256,512]{2,1,0:T(8,128)(2,1)S(1)}, bf16[2,256,512]{2,1,0:T(8,128)(2,1)}, u32[]{:S(2)}) copy-start(bf16[2,256,512]{2,1,0:T(8,128)(2,1)} %convolution_convert_fusion.1) | copy-start | bytes 1572868
  174.5 12.8 %copy-start.18 = (bf16[2,256,512]{2,1,0:T(8,128)(2,1)S(1)}, bf16[2,256,512]{2,1,0:T(8,128)(2,1)}, u32[]{:S(2)}) copy-start(bf16[2,256,512]{2,1,0:T(8,128)(2,1)} %convolution_convert_fusion.2) | copy-start | bytes 1572868
  193.2 850.0 %reduce-scatter.7.cloned.1.call-start = ((), (), s32[]{:S(2)}) async-start(), calls=%async_computation.6 | async-start | bytes 4718592 | tf_op jit(solution)/shard_map/reduce_scatter | solution.py:213
  200.9 249.4 %copy-start.23 = (f32[1024]{0:T(1024)S(1)}, f32[1024]{0:T(1024)}, u32[]{:S(2)}) copy-start(f32[1024]{0:T(1024)} %copy-done.22) | copy-start | bytes 12292
  200.9 249.4 %copy-start.29 = (f32[1024]{0:T(1024)S(1)}, f32[1024]{0:T(1024)}, u32[]{:S(2)}) copy-start(f32[1024]{0:T(1024)} %copy-done.28) | copy-start | bytes 12292
  201.0 940.5 %all-reduce.6.cloned.1.call-start = ((), (), s32[]{:S(2)}) async-start(), calls=%async_computation.10 | async-start | bytes 196608 | tf_op jit(solution)/shard_map/psum | solution.py:240
  202.0 262.4 %copy-start.21 = (f32[6144]{0:T(1024)}, f32[6144]{0:T(1024)S(1)}, u32[]{:S(2)}) copy-start(f32[6144]{0:T(1024)S(1)} %dynamic_update_slice.6) | copy-start | bytes 73732
  202.3 262.1 %copy-start.20 = (f32[8192]{0:T(1024)}, f32[8192]{0:T(1024)S(1)}, u32[]{:S(2)}) copy-start(f32[8192]{0:T(1024)S(1)} %dynamic_update_slice.7) | copy-start | bytes 98308
  450.3 14.8 %copy-start.35 = (f32[2048]{0:T(1024)S(1)}, f32[2048]{0:T(1024)}, u32[]{:S(2)}) copy-start(f32[2048]{0:T(1024)} %param.15) | copy-start | bytes 24580
  465.0 676.4 %reduce-scatter.5.cloned.1.call-start = ((), (), s32[]{:S(2)}) async-start(), calls=%async_computation.5 | async-start | bytes 14155776 | tf_op jit(solution)/shard_map/reduce_scatter | solution.py:212
  480.4 661.1 %reduce-scatter.11.cloned.1.call-start = ((), (), s32[]{:S(2)}) async-start(), calls=%async_computation.8 | async-start | bytes 18874368 | tf_op jit(solution)/shard_map/reduce_scatter | solution.py:215
  497.9 643.6 %reduce-scatter.9.cloned.1.call-start = ((), (), s32[]{:S(2)}) async-start(), calls=%async_computation.7 | async-start | bytes 18874368 | tf_op jit(solution)/shard_map/reduce_scatter | solution.py:214
  1012.2 16.2 %copy-start.32 = (f32[2048]{0:T(1024)S(1)}, f32[2048]{0:T(1024)}, u32[]{:S(2)}) copy-start(f32[2048]{0:T(1024)} %param.24) | copy-start | bytes 24580
  (28 other events, 153.0 us)
Sparse Core Ops, SparseCore 0:
  156.7 293.5 all-reduce.3
  451.8 560.3 all-gather.2
  1019.4 121.9 all-reduce.5
Sparse Core Ops, SparseCore 1:
  201.0 54.2 reduce-scatter.6
  480.5 90.1 reduce-scatter.4
  574.7 115.8 reduce-scatter.10
  694.7 116.0 reduce-scatter.8
